TPU v7x, 32 devices: a whole 2x2x4 slice. The times are simulated.
32 devices in a mesh: wide: 8 (over z, x), narrow: 4 (over y, core).
Axes of the slice: x: 2, y: 2, z: 4, core: 2. Of those that a mesh axis runs over, the one named last changes fastest.
Arguments:
- cost: float32 [1024, 16384], P('wide', 'narrow'), may hold values from 0 to 2
- plan: float32 [1024, 16384], P('wide', 'narrow'), may hold values from 0 to 2
- row_mass: float32 [1024], P('wide'), may hold values from 4096 to 28672
- col_mass: float32 [16384], P('narrow'), may hold values from 256 to 1792
- row_dual: float32 [1024], P('wide'), may hold values from -3 to 3
- col_dual: float32 [16384], P('narrow'), may hold values from -3 to 3
Outputs:
- plan_out: float32 [1024, 16384], P('wide', 'narrow')
- row_out: float32 [1024], P('wide')
- col_out: float32 [16384], P('narrow')
All inputs are finite; a program needn't handle non-finite values.
Results may differ from a plain program's by a relative error of at most 0.0001.
Values sent between devices are 32-bit elements; how exact they have to be, the bound alone decides.
A program may use at most 64 MiB of HBM per device.

v0:
```python
import math

import jax
import jax.numpy as jnp
from jax import lax
from jax.sharding import PartitionSpec as P

ITERS = 4


def shards(cost, plan, row_mass, col_mass, row_dual, col_dual):
    wide_count = lax.axis_size("wide")
    narrow_count = lax.axis_size("narrow")
    total_rows = plan.shape[0] * wide_count
    total_cols = plan.shape[1] * narrow_count
    step_base = 0.9 / math.sqrt(total_rows + total_cols)
    weight = jnp.float32(step_base)
    for step in range(ITERS):
        primal_step = step_base / weight
        dual_step = step_base * weight
        fresh = jnp.maximum(
            plan - primal_step * (cost - row_dual[:, None] - col_dual[None, :]), 0.0
        )
        change = fresh - plan
        extrap = fresh + change
        moved = jnp.sum(change * change)
        row_total = lax.psum(jnp.sum(extrap, axis=1), "narrow")
        new_row = row_dual + dual_step * (row_mass - row_total)
        row_square = jnp.sum((new_row - row_dual) ** 2)
        col_local = jnp.sum(extrap, axis=0)
        col_total = lax.psum(col_local, "wide")
        new_col = col_dual + dual_step * (col_mass - col_total)
        col_share = jnp.sum((new_col - col_dual) ** 2) / wide_count
        dual_share = row_square / narrow_count + col_share
        moved_all = lax.psum(moved, ("wide", "narrow"))
        dual_moved = lax.psum(dual_share, ("wide", "narrow"))
        weight = jnp.sqrt(weight * jnp.sqrt((dual_moved + 1.0) / (moved_all + 1.0)))
        plan, row_dual, col_dual = (fresh, new_row, new_col)
    return (plan, row_dual, col_dual)


def solution(mesh):
    in_specs = (
        P("wide", "narrow"),
        P("wide", "narrow"),
        P("wide"),
        P("narrow"),
        P("wide"),
        P("narrow"),
    )
    out_specs = (P("wide", "narrow"), P("wide"), P("narrow"))
    return jax.shard_map(shards, mesh=mesh, in_specs=in_specs, out_specs=out_specs, check_vma=False)
```

profile of v0, /device:TPU:0, one launch (start us, length us, event | category | flops | bytes accessed | tf_op | source)
XLA Modules:
  0.0 314.4 jit_solution(7714371782723744070)
XLA Ops:
  0.6 0.0 copy-start.1
  0.6 0.0 copy-start.3
  0.7 0.0 copy-start.2
  0.7 0.0 copy-start.4
  0.7 0.0 copy-start
  0.7 4.2 %multiply_reduce_fusion.2 = (f32[]{:T(128)}, f32[4096]{0:T(1024)S(1)}, f32[128]{0:T(128)S(1)}) fusion(f32[128,4096]{1,0:T(8,128)} %param.7, f32[4096]{0:T(1024)} %param.11, f32[128,4096]{1,0:T(8,128)} %param.6, f32[128]{0:T(128)} %param.10), kind=kLoop, calls=%fused_computation.6 | loop fusion | flops 5238655 | bytes 4228100 | tf_op jit(solution)/shard_map/reduce_sum | solution.py:26
  4.9 38.8 %psum.99 = f32[4096]{0:T(1024)S(1)} all-reduce(f32[4096]{0:T(1024)S(1)} %get-tuple-element.12), channel_id=1, replica_groups=mesh['wide'=8,'narrow'=4] {'wide'}, use_global_device_ids=true, to_apply=%region_4.0 | all-reduce | flops 4096 | bytes 32768 | tf_op jit(solution)/shard_map/psum | solution.py:31
  43.7 5.6 %psum.98 = f32[128]{0:T(128)S(1)} all-reduce(f32[128]{0:T(128)S(1)} %get-tuple-element.13), channel_id=1, replica_groups=mesh['wide'=8,'narrow'=4] {'narrow'}, use_global_device_ids=true, to_apply=%region_1.0 | all-reduce | flops 128 | bytes 1024 | tf_op jit(solution)/shard_map/psum | solution.py:27
  49.3 0.0 copy-done.3
  49.3 0.0 copy-done.4
  49.3 0.6 multiply_reduce_fusion.8
  50.6 0.0 copy-done.1
  50.6 0.0 copy-done.2
  50.6 0.6 multiply_reduce_fusion.5
  51.9 37.2 %all-reduce.2 = (f32[]{:T(128)}, f32[]{:T(128)}) all-reduce(f32[]{:T(128)S(6)} %add.94, f32[]{:T(128)} %get-tuple-element.11), channel_id=1, replica_groups=mesh['wide'=8,'narrow'=4] {'wide','narrow'}, use_global_device_ids=true, to_apply=%region_6.0 | all-reduce | flops 2 | bytes 16 | tf_op jit(solution)/shard_map/psum | solution.py:36
  90.5 0.0 copy-done
  90.5 3.7 %multiply_reduce_fusion.1 = (f32[]{:T(128)}, f32[128]{0:T(128)S(1)}, f32[4096]{0:T(1024)S(1)}) fusion(f32[4096]{0:T(1024)S(1)} %get-tuple-element.30, f32[128,4096]{1,0:T(8,128)} %param.6, f32[128]{0:T(128)S(1)} %get-tuple-element.32, f32[]{:T(128)S(6)} %div.39, f32[128,4096]{1,0:T(8,128)S(1)} %copy-done, f32[4096]{0:T(1024)S(1)} %copy-done.1, ...), kind=kLoop, calls=%fused_computation.4 | loop fusion | flops 7860095 | bytes 4245000 | tf_op jit(solution)/shard_map/reduce_sum | solution.py:26
  94.2 6.9 %psum.102 = f32[128]{0:T(128)S(1)} all-reduce(f32[128]{0:T(128)S(1)} %get-tuple-element.9), channel_id=1, replica_groups=mesh['wide'=8,'narrow'=4] {'narrow'}, use_global_device_ids=true, to_apply=%region_10.0 | all-reduce | flops 128 | bytes 1024 | tf_op jit(solution)/shard_map/psum | solution.py:27
  101.1 0.6 multiply_reduce_fusion.7
  102.4 35.6 %psum.103 = f32[4096]{0:T(1024)S(1)} all-reduce(f32[4096]{0:T(1024)S(1)} %get-tuple-element.10), channel_id=1, replica_groups=mesh['wide'=8,'narrow'=4] {'wide'}, use_global_device_ids=true, to_apply=%region_13.0 | all-reduce | flops 4096 | bytes 32768 | tf_op jit(solution)/shard_map/psum | solution.py:31
  138.0 0.6 multiply_reduce_fusion.4
  139.2 37.1 %all-reduce.1 = (f32[]{:T(128)}, f32[]{:T(128)}) all-reduce(f32[]{:T(128)S(6)} %add.100, f32[]{:T(128)} %get-tuple-element.8), channel_id=1, replica_groups=mesh['wide'=8,'narrow'=4] {'wide','narrow'}, use_global_device_ids=true, to_apply=%region_15.0 | all-reduce | flops 2 | bytes 16 | tf_op jit(solution)/shard_map/psum | solution.py:36
  177.8 4.2 %multiply_reduce_fusion = (f32[]{:T(128)}, f32[128]{0:T(128)S(1)}, f32[4096]{0:T(1024)S(1)}) fusion(f32[4096]{0:T(1024)S(1)} %get-tuple-element.26, f32[128,4096]{1,0:T(8,128)} %param.6, f32[128]{0:T(128)S(1)} %get-tuple-element.28, f32[]{:T(128)S(6)} %div.43, f32[4096]{0:T(1024)S(1)} %get-tuple-element.30, f32[128]{0:T(128)S(1)} %get-tuple-element.32, ...), kind=kLoop, calls=%fused_computation.2 | loop fusion | flops 10481535 | bytes 4261900 | tf_op jit(solution)/shard_map/reduce_sum | solution.py:26
  182.0 7.2 %psum.106 = f32[128]{0:T(128)S(1)} all-reduce(f32[128]{0:T(128)S(1)} %get-tuple-element.6), channel_id=1, replica_groups=mesh['wide'=8,'narrow'=4] {'narrow'}, use_global_device_ids=true, to_apply=%region_19.0 | all-reduce | flops 128 | bytes 1024 | tf_op jit(solution)/shard_map/psum | solution.py:27
  189.2 0.6 multiply_reduce_fusion.6
  190.5 35.3 %psum.107 = f32[4096]{0:T(1024)S(1)} all-reduce(f32[4096]{0:T(1024)S(1)} %get-tuple-element.7), channel_id=1, replica_groups=mesh['wide'=8,'narrow'=4] {'wide'}, use_global_device_ids=true, to_apply=%region_22.0 | all-reduce | flops 4096 | bytes 32768 | tf_op jit(solution)/shard_map/psum | solution.py:31
  225.8 0.6 multiply_reduce_fusion.3
  227.0 37.3 %all-reduce = (f32[]{:T(128)}, f32[]{:T(128)}) all-reduce(f32[]{:T(128)S(6)} %add.106, f32[]{:T(128)} %get-tuple-element.5), channel_id=1, replica_groups=mesh['wide'=8,'narrow'=4] {'wide','narrow'}, use_global_device_ids=true, to_apply=%region_24.0 | all-reduce | flops 2 | bytes 16 | tf_op jit(solution)/shard_map/psum | solution.py:36
  265.8 4.9 %fusion.6 = (f32[4096]{0:T(1024)S(1)}, f32[128]{0:T(128)S(1)}, f32[128,4096]{1,0:T(8,128)}) fusion(f32[4096]{0:T(1024)S(1)} %get-tuple-element.26, f32[128,4096]{1,0:T(8,128)} %param.6, f32[128]{0:T(128)S(1)} %get-tuple-element.28, f32[]{:T(128)S(6)} %div.43, f32[4096]{0:T(1024)S(1)} %get-tuple-element.30, f32[128]{0:T(128)S(1)} %get-tuple-element.32, ...), kind=kLoop, calls=%fused_computation.17 | loop fusion | flops 12054400 | bytes 6375948 | tf_op jit(solution)/shard_map/reduce_sum | solution.py:30
  270.7 36.8 %psum.111 = f32[4096]{0:T(1024)S(1)} all-reduce(f32[4096]{0:T(1024)S(1)} %get-tuple-element.3), channel_id=1, replica_groups=mesh['wide'=8,'narrow'=4] {'wide'}, use_global_device_ids=true, to_apply=%region_30.0 | all-reduce | flops 4096 | bytes 32768 | tf_op jit(solution)/shard_map/psum | solution.py:31
  307.5 0.6 multiply_add_fusion
  308.1 5.7 %psum.110 = f32[128]{0:T(128)S(1)} all-reduce(f32[128]{0:T(128)S(1)} %get-tuple-element.4), channel_id=1, replica_groups=mesh['wide'=8,'narrow'=4] {'narrow'}, use_global_device_ids=true, to_apply=%region_28.0 | all-reduce | flops 128 | bytes 1024 | tf_op jit(solution)/shard_map/psum | solution.py:27
  313.9 0.5 multiply_add_fusion.4
Async XLA Ops:
  0.6 49.9 %copy-start.1 = (f32[4096]{0:T(1024)S(1)}, f32[4096]{0:T(1024)}, u32[]{:S(2)}) copy-start(f32[4096]{0:T(1024)} %param.11) | copy-start | bytes 49156
  0.6 48.7 %copy-start.3 = (f32[128]{0:T(128)S(1)}, f32[128]{0:T(128)}, u32[]{:S(2)}) copy-start(f32[128]{0:T(128)} %param.10) | copy-start | bytes 1540
  0.7 49.9 %copy-start.2 = (f32[4096]{0:T(1024)S(1)}, f32[4096]{0:T(1024)}, u32[]{:S(2)}) copy-start(f32[4096]{0:T(1024)} %param.9) | copy-start | bytes 49156
  0.7 48.7 %copy-start.4 = (f32[128]{0:T(128)S(1)}, f32[128]{0:T(128)}, u32[]{:S(2)}) copy-start(f32[128]{0:T(128)} %param.8) | copy-start | bytes 1540
  0.7 89.8 %copy-start = (f32[128,4096]{1,0:T(8,128)S(1)}, f32[128,4096]{1,0:T(8,128)}, u32[]{:S(2)}) copy-start(f32[128,4096]{1,0:T(8,128)} %param.7) | copy-start | bytes 6291460
where the time goes:
time: 315 us; the launch traced here: 314 us
  blocking collectives  284 us (90%)
  other arithmetic  21.7 us (7%)
  between operations  9.03 us (3%)
    psum x4, blocking collectives, shards(): col_total = lax.psum(col_local, 'wide')  147 us
    psum x3, blocking collectives, shards(): dual_moved = lax.psum(dual_share, ('wide', 'narrow'))  112 us
    psum x4, blocking collectives, shards(): row_total = lax.psum(jnp.sum(extrap, axis=1), 'narrow')  25.5 us
    reduce_sum x3, other arithmetic, shards(): moved = jnp.sum(change * change)  12.1 us

commit v1 on v0

v1 whole, which is shorter than its diff:
```python
import functools
import math

import jax
import jax.numpy as jnp
from jax import lax
from jax.experimental import pallas as pl
from jax.experimental.pallas import tpu as pltpu
from jax.sharding import PartitionSpec as P

ITERS = 4
LANES = 128
BLOCKS = 8
MESH = pl.DeviceIdType.MESH


def kernel(
    W, N, G, step_base,
    cost_hbm, plan_hbm, rmass_ref, cmass_ref, u_ref, v_ref,
    plan_out, u_out, v_out,
    cost, plan, colbuf, ub, ucur, V, SB, RB, RP, RH, SC,
    in_sem, out_sem,
    s1_send, s1_recv, row_send, row_recv, rho_send, rho_recv,
    v_send, v_recv, sc_send, sc_recv,
):
    rows, cols = plan.shape
    chunks = cols // LANES
    part = chunks // G
    per_block = chunks // BLOCKS
    width = per_block * LANES
    w = lax.axis_index("wide")
    n = lax.axis_index("narrow")
    h = lax.rem(w, G)
    base = w - h

    loads = []
    for b in range(BLOCKS):
        sl = (slice(None), pl.ds(b * width, width))
        pair = (
            pltpu.make_async_copy(cost_hbm.at[sl], cost.at[sl], in_sem.at[0, b]),
            pltpu.make_async_copy(plan_hbm.at[sl], plan.at[sl], in_sem.at[1, b]),
        )
        for copy in pair:
            copy.start()
        loads.append(pair)

    wide_peers = [(lax.rem(w + d, W), lax.rem(w + W - d, W)) for d in range(1, W)]
    narrow_peers = [(lax.rem(n + d, N), lax.rem(n + N - d, N)) for d in range(1, N)]
    block_peers = []
    for dh in range(G):
        for dn in range(N):
            if dh == 0 and dn == 0:
                continue
            hp, hs = lax.rem(h + dh, G), lax.rem(h + G - dh, G)
            np_, ns = lax.rem(n + dn, N), lax.rem(n + N - dn, N)
            block_peers.append((dh, dn, hp, np_, hs, ns))

    barrier = pltpu.get_barrier_semaphore()
    greeted = 0
    for to, _ in wide_peers:
        pl.semaphore_signal(barrier, inc=1, device_id=(to, n), device_id_type=MESH)
        greeted += 1
    for to, _ in narrow_peers:
        pl.semaphore_signal(barrier, inc=1, device_id=(w, to), device_id_type=MESH)
        greeted += 1
    for dh, dn, hp, np_, _, _ in block_peers:
        if dh and dn:
            pl.semaphore_signal(barrier, inc=1, device_id=(base + hp, np_), device_id_type=MESH)
            greeted += 1

    def spread(row):
        return jnp.broadcast_to(row, (LANES, LANES)).T

    def to_lanes(acc):
        return jnp.concatenate(
            [
                jnp.sum(acc[g * LANES:(g + 1) * LANES].T, axis=0, keepdims=True)
                for g in range(rows // LANES)
            ],
            axis=0,
        )

    for g in range(rows // LANES):
        ub[g * LANES:(g + 1) * LANES, :] = spread(u_ref[g:g + 1, :])
    ucur[...] = u_ref[...]
    for g in range(G):
        V[0, g] = v_ref[g * part:(g + 1) * part, :]

    weight = jnp.full((1, 1), step_base, jnp.float32)
    pending = []
    stores = []
    for k in range(ITERS):
        last = k == ITERS - 1
        primal = step_base / weight
        dual = step_base * weight
        tau = jnp.broadcast_to(primal, (1, LANES))

        def chunk(c, carry, k=k, tau=tau):
            racc, macc = carry
            lanes = pl.ds(pl.multiple_of(c * LANES, LANES), LANES)
            x = plan[:, lanes]
            g, r = c // part, c % part
            v = V[k, g, pl.ds(r, 1), :]
            f = jnp.maximum(x - tau * (cost[:, lanes] - ub[...] - v), 0.0)
            ch = f - x
            plan[:, lanes] = f
            ext = f + ch
            colbuf[pl.ds(c, 1), :] = jnp.sum(ext, axis=0, keepdims=True)
            sq = ch * ch
            return racc + ext, macc + jnp.sum(sq.reshape(rows // 8, 8, LANES), axis=0)

        carry = (jnp.zeros((rows, LANES), jnp.float32), jnp.zeros((8, LANES), jnp.float32))
        if k == 0:
            for b in range(BLOCKS):
                for copy in loads[b]:
                    copy.wait()
                carry = lax.fori_loop(b * per_block, (b + 1) * per_block, chunk, carry, unroll=2)
        elif last:
            for b in range(BLOCKS):
                carry = lax.fori_loop(b * per_block, (b + 1) * per_block, chunk, carry, unroll=2)
                sl = (slice(None), pl.ds(b * width, width))
                copy = pltpu.make_async_copy(plan.at[sl], plan_out.at[sl], out_sem.at[b])
                copy.start()
                stores.append(copy)
        else:
            carry = lax.fori_loop(0, chunks, chunk, carry, unroll=2)
        racc, macc = carry

        moved_row = jnp.sum(macc, axis=0, keepdims=True)
        for g in range(G):
            SB[k, g, 0:part, :] = colbuf[g * part:(g + 1) * part, :]
            SB[k, g, part:part + 1, :] = moved_row
        if k == 0:
            pl.semaphore_wait(barrier, greeted)
        waits1 = []
        for d, (to, src) in enumerate(wide_peers):
            copy = pltpu.make_async_remote_copy(
                src_ref=SB.at[k, lax.rem(to, G)], dst_ref=RB.at[k, w],
                send_sem=s1_send.at[k, d], recv_sem=s1_recv.at[k, w],
                device_id=(to, n), device_id_type=MESH)
            copy.start()
            pending.append(copy)
            waits1.append(pltpu.make_async_remote_copy(
                src_ref=SB.at[k, 0], dst_ref=RB.at[k, src],
                send_sem=s1_send.at[k, d], recv_sem=s1_recv.at[k, src],
                device_id=(to, n), device_id_type=MESH))
        RP[k, n] = to_lanes(racc)
        waits = []
        for d, (to, src) in enumerate(narrow_peers):
            copy = pltpu.make_async_remote_copy(
                src_ref=RP.at[k, n], dst_ref=RP.at[k, n],
                send_sem=row_send.at[k, d], recv_sem=row_recv.at[k, n],
                device_id=(w, to), device_id_type=MESH)
            copy.start()
            pending.append(copy)
            waits.append(pltpu.make_async_remote_copy(
                src_ref=RP.at[k, src], dst_ref=RP.at[k, src],
                send_sem=row_send.at[k, d], recv_sem=row_recv.at[k, src],
                device_id=(w, to), device_id_type=MESH))
        RB[k, w] = SB[k, h]
        for copy in waits:
            copy.wait_recv()
        total = RP[k, 0]
        for i in range(1, N):
            total = total + RP[k, i]
        u_old = ucur[...]
        u_new = u_old + dual * (rmass_ref[...] - total)
        if last:
            u_out[...] = u_new
        else:
            rho = jnp.sum((u_new - u_old) ** 2, axis=0, keepdims=True)
            RH[k, w] = rho
            waits_rho = []
            for d, (to, src) in enumerate(wide_peers):
                copy = pltpu.make_async_remote_copy(
                    src_ref=RH.at[k, w], dst_ref=RH.at[k, w],
                    send_sem=rho_send.at[k, d], recv_sem=rho_recv.at[k, w],
                    device_id=(to, n), device_id_type=MESH)
                copy.start()
                pending.append(copy)
                waits_rho.append(pltpu.make_async_remote_copy(
                    src_ref=RH.at[k, src], dst_ref=RH.at[k, src],
                    send_sem=rho_send.at[k, d], recv_sem=rho_recv.at[k, src],
                    device_id=(to, n), device_id_type=MESH))
            ucur[...] = u_new
            for g in range(rows // LANES):
                ub[g * LANES:(g + 1) * LANES, :] = spread(u_new[g:g + 1, :])

        for copy in waits1:
            copy.wait_recv()
        both = RB[k, 0]
        for i in range(1, W):
            both = both + RB[k, i]
        v_old = V[k, h]
        mass = cmass_ref[pl.ds(pl.multiple_of(h * part, part), part), :]
        v_new = v_old + dual * (mass - both[0:part])
        V[k + 1, h] = v_new
        v_waits = []
        sc_waits = []
        if not last:
            mine = h * N + n
            SC[k, mine, 0:1, :] = jnp.sum((v_new - v_old) ** 2, axis=0, keepdims=True)
            SC[k, mine, 1:2, :] = both[part:part + 1]
        for i, (dh, dn, hp, np_, hs, ns) in enumerate(block_peers):
            if dh and dn == 0:
                copy = pltpu.make_async_remote_copy(
                    src_ref=V.at[k + 1, h], dst_ref=V.at[k + 1, h],
                    send_sem=v_send.at[k, dh], recv_sem=v_recv.at[k, h],
                    device_id=(base + hp, n), device_id_type=MESH)
                copy.start()
                pending.append(copy)
                v_waits.append(pltpu.make_async_remote_copy(
                    src_ref=V.at[k + 1, hs], dst_ref=V.at[k + 1, hs],
                    send_sem=v_send.at[k, dh], recv_sem=v_recv.at[k, hs],
                    device_id=(base + hp, n), device_id_type=MESH))
            if not last:
                theirs = hs * N + ns
                copy = pltpu.make_async_remote_copy(
                    src_ref=SC.at[k, mine], dst_ref=SC.at[k, mine],
                    send_sem=sc_send.at[k, i], recv_sem=sc_recv.at[k, mine],
                    device_id=(base + hp, np_), device_id_type=MESH)
                copy.start()
                pending.append(copy)
                sc_waits.append(pltpu.make_async_remote_copy(
                    src_ref=SC.at[k, theirs], dst_ref=SC.at[k, theirs],
                    send_sem=sc_send.at[k, i], recv_sem=sc_recv.at[k, theirs],
                    device_id=(base + hp, np_), device_id_type=MESH))
        if not last:
            for copy in waits_rho:
                copy.wait_recv()
            squares = RH[k, 0]
            for i in range(1, W):
                squares = squares + RH[k, i]
            for copy in sc_waits:
                copy.wait_recv()
            for i in range(G * N):
                squares = squares + SC[k, i, 0:1, :]
            moved = SC[k, 0, 1:2, :]
            for i in range(1, N):
                moved = moved + SC[k, i, 1:2, :]
            dual_moved = jnp.sum(squares, axis=1, keepdims=True)
            moved = jnp.sum(moved, axis=1, keepdims=True)
            weight = jnp.sqrt(weight * jnp.sqrt((dual_moved + 1.0) / (moved + 1.0)))
        for copy in v_waits:
            copy.wait_recv()
    for g in range(G):
        v_out[g * part:(g + 1) * part, :] = V[ITERS, g]
    for copy in pending:
        copy.wait_send()
    for copy in stores:
        copy.wait()


def shards(W, N, G, cost, plan, row_mass, col_mass, row_dual, col_dual):
    rows, cols = plan.shape
    step_base = 0.9 / math.sqrt(rows * W + cols * N)
    chunks = cols // LANES
    part = chunks // G
    groups = rows // LANES
    f32 = jnp.float32
    dma = pltpu.SemaphoreType.DMA
    vmem = pl.BlockSpec(memory_space=pltpu.VMEM)
    hbm = pl.BlockSpec(memory_space=pl.ANY)
    plan_out, u_out, v_out = pl.pallas_call(
        functools.partial(kernel, W, N, G, step_base),
        out_shape=(
            jax.ShapeDtypeStruct((rows, cols), f32),
            jax.ShapeDtypeStruct((groups, LANES), f32),
            jax.ShapeDtypeStruct((chunks, LANES), f32),
        ),
        in_specs=[hbm, hbm, vmem, vmem, vmem, vmem],
        out_specs=(hbm, vmem, vmem),
        scratch_shapes=[
            pltpu.VMEM((rows, cols), f32),
            pltpu.VMEM((rows, cols), f32),
            pltpu.VMEM((chunks, LANES), f32),
            pltpu.VMEM((rows, LANES), f32),
            pltpu.VMEM((groups, LANES), f32),
            pltpu.VMEM((ITERS + 1, G, part, LANES), f32),
            pltpu.VMEM((ITERS, G, part + 1, LANES), f32),
            pltpu.VMEM((ITERS, W, part + 1, LANES), f32),
            pltpu.VMEM((ITERS, N, groups, LANES), f32),
            pltpu.VMEM((ITERS, W, 1, LANES), f32),
            pltpu.VMEM((ITERS, G * N, 2, LANES), f32),
            dma((2, BLOCKS)), dma((BLOCKS,)),
            dma((ITERS, W)), dma((ITERS, W)),
            dma((ITERS, N)), dma((ITERS, N)),
            dma((ITERS, W)), dma((ITERS, W)),
            dma((ITERS, G)), dma((ITERS, G)),
            dma((ITERS, G * N)), dma((ITERS, G * N)),
        ],
        compiler_params=pltpu.CompilerParams(collective_id=0, has_side_effects=True),
        name="pdhg",
    )(
        cost, plan,
        row_mass.reshape(groups, LANES), col_mass.reshape(chunks, LANES),
        row_dual.reshape(groups, LANES), col_dual.reshape(chunks, LANES),
    )
    return plan_out, u_out.reshape(rows), v_out.reshape(cols)


def solution(mesh):
    W, N = mesh.shape["wide"], mesh.shape["narrow"]
    G = 2 if W % 2 == 0 else 1
    in_specs = (
        P("wide", "narrow"),
        P("wide", "narrow"),
        P("wide"),
        P("narrow"),
        P("wide"),
        P("narrow"),
    )
    out_specs = (P("wide", "narrow"), P("wide"), P("narrow"))
    return jax.shard_map(
        functools.partial(shards, W, N, G),
        mesh=mesh, in_specs=in_specs, out_specs=out_specs, check_vma=False)
```

time: 315 us -> 49.1 us (0.16)
  blocking collectives: 284 us -> 0 us
  Pallas kernels: 0 us -> 43.9 us
  other arithmetic: 21.7 us -> 0 us
  between operations: 9.03 us -> 0.66 us
  local copies, waits for them, and re-layouts: 0.02 us -> 4.24 us
    psum x11 -> x0, blocking collectives: 284 us -> none  [the longest x4 147 us: shards(): col_total = lax.psum(col_local, 'wide')]
    pallas_call x0 -> x1, Pallas kernels: none -> 43.9 us  [shards(): pl.pallas_call(functools.partial(kernel, W, N, G, step_base), out_shape=(...]
    reduce_sum x10 -> x0, other arithmetic: 20.6 us -> none  [the longest x3 12.1 us: shards(): moved = jnp.sum(change * change)]
    unnamed x10 -> x7, local copies, waits for them, and re-layouts: 0.02 us -> 4.24 us
where the time goes in v1:
time: 49.1 us; the launch traced here: 48.8 us
  Pallas kernels  43.9 us (89%)
  local copies, waits for them, and re-layouts  4.24 us (9%)
  between operations  0.66 us (1%)
    pallas_call x1, Pallas kernels, shards(): pl.pallas_call(functools.partial(kernel, W, N, G, step_base), out_shape=(...  43.9 us
    unnamed x7, local copies, waits for them, and re-layouts  4.24 us

profile of v1, /device:TPU:0, one launch (start us, length us, event | category | flops | bytes accessed | tf_op | source)
XLA Modules:
  0.0 48.8 jit_solution(7301942987942507598)
XLA Ops:
  0.6 43.9 %pdhg.1 = (f32[128,4096]{1,0:T(8,128)}, f32[1,128]{1,0:T(1,128)}, f32[32,128]{1,0:T(8,128)}) custom-call(f32[128,4096]{1,0:T(8,128)} %cost_hbm.1, f32[128,4096]{1,0:T(8,128)} %plan_hbm.1, f32[1,128]{1,0:T(1,128)} %bitcast.9, f32[32,128]{1,0:T(8,128)} %bitcast.6, f32[1,128]{1,0:T(1,128)} %bitcast.10, f32[32,128]{1,0:T(8,128)} %bitcast.7), custom_call_target="tpu_custom_call" | custom-call | tf_op jit(solution)/shard_map/pdhg/pallas_call | solution.py:264
  44.5 0.0 copy-start.1
  44.5 0.0 copy-start
  44.5 3.1 %copy.12 = f32[128,4096]{1,0:T(8,128)} copy(f32[128,4096]{1,0:T(8,128)} %get-tuple-element.12) | data formatting | bytes 4194304
  47.7 0.0 copy-done.1
  47.7 0.5 %copy.13 = f32[128]{0:T(128)} copy(f32[128]{0:T(128)S(1)} %bitcast.11) | data formatting | bytes 1024
  48.2 0.0 copy-done
  48.2 0.6 %copy.14 = f32[4096]{0:T(1024)} copy(f32[4096]{0:T(1024)S(1)} %bitcast.8) | data formatting | bytes 32768
Async XLA Ops:
  44.5 3.1 %copy-start.1 = (f32[1,128]{1,0:T(1,128)S(1)}, f32[1,128]{1,0:T(1,128)}, u32[]{:S(2)}) copy-start(f32[1,128]{1,0:T(1,128)} %get-tuple-element.7) | copy-start | bytes 1540
  44.5 3.6 %copy-start = (f32[32,128]{1,0:T(8,128)S(1)}, f32[32,128]{1,0:T(8,128)}, u32[]{:S(2)}) copy-start(f32[32,128]{1,0:T(8,128)} %get-tuple-element.8) | copy-start | bytes 49156

commit v2 on v0

v2 whole, which is shorter than its diff:
```python
import functools
import math

import jax
import jax.numpy as jnp
from jax import lax
from jax.experimental import pallas as pl
from jax.experimental.pallas import tpu as pltpu
from jax.sharding import PartitionSpec as P

ITERS = 4
LANES = 128
BLOCKS = 8
MESH = pl.DeviceIdType.MESH


def exchange(ref, k, mine, peers, send_sem, recv_sem, source=None):
    sent, waits = [], []
    for d, (to, src, device) in enumerate(peers):
        copy = pltpu.make_async_remote_copy(
            src_ref=ref.at[k, mine] if source is None else source, dst_ref=ref.at[k, mine],
            send_sem=send_sem.at[k, d], recv_sem=recv_sem.at[k, mine],
            device_id=device, device_id_type=MESH)
        copy.start()
        sent.append(copy)
        waits.append(pltpu.make_async_remote_copy(
            src_ref=ref.at[k, src], dst_ref=ref.at[k, src],
            send_sem=send_sem.at[k, d], recv_sem=recv_sem.at[k, src],
            device_id=device, device_id_type=MESH))
    return sent, waits


def arrived(waits):
    for copy in waits:
        copy.wait_recv()


def total_of(ref, k, count):
    out = ref[k, 0]
    for i in range(1, count):
        out = out + ref[k, i]
    return out


def kernel(
    W, N, step_base,
    cost_hbm, plan_hbm, rmass_hbm, cmass_hbm, u_hbm, v_hbm,
    plan_out, u_out, v_out,
    cost, plan_a, plan_b, gap, rmass, cmass, ub, ucur, V, CB, RB, RP, RH, MV, SC,
    in_sem, small_sem,
    s1_send, s1_recv, row_send, row_recv, rho_send, rho_recv,
    mv_send, mv_recv, sc_send, sc_recv,
):
    rows, cols = plan_a.shape
    chunks = cols // LANES
    groups = rows // LANES
    per_block = chunks // BLOCKS
    width = per_block * LANES
    w = lax.axis_index("wide")
    n = lax.axis_index("narrow")

    wide_peers = []
    for d in range(W - 1, 0, -1):
        to = lax.rem(w + d, W)
        wide_peers.append((to, lax.rem(w + W - d, W), (to, n)))
    narrow_peers = []
    for d in range(N - 1, 0, -1):
        to = lax.rem(n + d, N)
        narrow_peers.append((to, lax.rem(n + N - d, N), (w, to)))

    barrier = pltpu.get_barrier_semaphore()
    for _, _, device in wide_peers + narrow_peers:
        pl.semaphore_signal(barrier, inc=1, device_id=device, device_id_type=MESH)

    smalls = [
        pltpu.make_async_copy(u_hbm, ucur, small_sem.at[0]),
        pltpu.make_async_copy(v_hbm, V.at[0], small_sem.at[1]),
        pltpu.make_async_copy(rmass_hbm, rmass, small_sem.at[2]),
        pltpu.make_async_copy(cmass_hbm, cmass, small_sem.at[3]),
    ]
    for copy in smalls:
        copy.start()
    loads = []
    for b in range(BLOCKS):
        sl = (slice(None), pl.ds(b * width, width))
        pair = (
            pltpu.make_async_copy(cost_hbm.at[sl], cost.at[sl], in_sem.at[0, b]),
            pltpu.make_async_copy(plan_hbm.at[sl], plan_a.at[sl], in_sem.at[1, b]),
        )
        for copy in pair:
            copy.start()
        loads.append(pair)

    def spread(u):
        for g in range(groups):
            ub[g * LANES:(g + 1) * LANES, :] = jnp.broadcast_to(u[g:g + 1], (LANES, LANES)).T

    def to_lanes(acc):
        return jnp.concatenate(
            [
                jnp.sum(acc[g * LANES:(g + 1) * LANES].T, axis=0, keepdims=True)
                for g in range(groups)
            ],
            axis=0,
        )

    def lanes_of(c):
        return pl.ds(pl.multiple_of(c * LANES, LANES), LANES)

    for copy in smalls:
        copy.wait()
    spread(ucur[...])

    zero_rows = jnp.zeros((rows, LANES), jnp.float32)
    weight = jnp.full((1, 1), step_base, jnp.float32)
    row_old = None
    pending = []
    for k in range(ITERS):
        last = k == ITERS - 1
        old = plan_a if k % 2 == 0 else plan_b
        new = plan_out if last else (plan_b if k % 2 == 0 else plan_a)
        dual = step_base * weight
        tau = jnp.broadcast_to(step_base / weight, (1, LANES))

        if k == 0:
            def first(c, racc, old=old, new=new, tau=tau):
                lanes = lanes_of(c)
                x = old[:, lanes]
                f = jnp.maximum(
                    x - tau * (cost[:, lanes] - ub[...] - V[0, pl.ds(c, 1), :]), 0.0)
                new[:, lanes] = f
                ext = f + (f - x)
                CB[0, pl.ds(c, 1), :] = jnp.sum(ext, axis=0, keepdims=True)
                return racc + ext

            racc = zero_rows
            for b in range(BLOCKS):
                for copy in loads[b]:
                    copy.wait()
                racc = lax.fori_loop(
                    b * per_block, (b + 1) * per_block, first, racc, unroll=2)
            RB[0, w] = CB[0]
            pl.semaphore_wait(barrier, W - 1 + N - 1)
        else:
            def step(c, racc, k=k, old=old, new=new, tau=tau):
                lanes = lanes_of(c)
                f = jnp.maximum(old[:, lanes] - tau * gap[:, lanes], 0.0)
                new[:, lanes] = f
                CB[k + 1, pl.ds(c, 1), :] = jnp.sum(f, axis=0, keepdims=True)
                return racc + f

            racc = lax.fori_loop(0, chunks, step, zero_rows, unroll=4)
            RB[k, w] = 2.0 * CB[k + 1] - CB[k]

        sent, col_waits = exchange(RB, k, w, wide_peers, s1_send, s1_recv)
        pending += sent
        row_new = to_lanes(racc)
        RP[k, n] = row_new if k == 0 else 2.0 * row_new - row_old
        row_old = row_new
        sent, row_waits = exchange(RP, k, n, narrow_peers, row_send, row_recv)
        pending += sent

        if not last:
            def change(c, carry, k=k, old=old, new=new):
                lanes = lanes_of(c)
                f = new[:, lanes]
                ch = f - old[:, lanes]
                sq = jnp.sum((ch * ch).reshape(rows // 8, 8, LANES), axis=0)
                if k:
                    return (carry[0] + sq,)
                CB[1, pl.ds(c, 1), :] = jnp.sum(f, axis=0, keepdims=True)
                return carry[0] + sq, carry[1] + f

            start = (jnp.zeros((8, LANES), jnp.float32),)
            out = lax.fori_loop(
                0, chunks, change, start if k else start + (zero_rows,), unroll=2)
            MV[k, w] = jnp.sum(out[0], axis=0, keepdims=True)
            sent, mv_waits = exchange(MV, k, w, wide_peers, mv_send, mv_recv)
            pending += sent
            if k == 0:
                row_old = to_lanes(out[1])

        arrived(row_waits)
        u_old = ucur[...]
        u_new = u_old + dual * (rmass[...] - total_of(RP, k, N))
        if last:
            u_out[...] = u_new
        else:
            RH[k, w] = jnp.sum((u_new - u_old) ** 2, axis=0, keepdims=True)
            sent, rho_waits = exchange(RH, k, w, wide_peers, rho_send, rho_recv)
            pending += sent
            ucur[...] = u_new
            spread(u_new)
            arrived(mv_waits)
            SC[k, n, 1:2, :] = total_of(MV, k, W)

        arrived(col_waits)
        v_old = V[k]
        v_new = v_old + dual * (cmass[...] - total_of(RB, k, W))
        if last:
            v_out[...] = v_new
            continue
        SC[k, n, 0:1, :] = jnp.sum((v_new - v_old) ** 2, axis=0, keepdims=True)
        V[k + 1] = v_new
        sent, sc_waits = exchange(SC, k, n, narrow_peers, sc_send, sc_recv)
        pending += sent

        def reduce_cost(c, carry, k=k):
            lanes = lanes_of(c)
            gap[:, lanes] = cost[:, lanes] - ub[...] - V[k + 1, pl.ds(c, 1), :]
            return carry

        lax.fori_loop(0, chunks, reduce_cost, 0, unroll=2)
        arrived(rho_waits)
        rho = total_of(RH, k, W)
        arrived(sc_waits)
        both = total_of(SC, k, N)
        dual_moved = jnp.sum(rho + both[0:1], axis=1, keepdims=True)
        moved = jnp.sum(both[1:2], axis=1, keepdims=True)
        weight = jnp.sqrt(weight * jnp.sqrt((dual_moved + 1.0) / (moved + 1.0)))
    for copy in pending:
        copy.wait_send()


def shards(W, N, cost, plan, row_mass, col_mass, row_dual, col_dual):
    rows, cols = plan.shape
    step_base = 0.9 / math.sqrt(rows * W + cols * N)
    chunks = cols // LANES
    groups = rows // LANES
    f32 = jnp.float32
    dma = pltpu.SemaphoreType.DMA
    vmem = pl.BlockSpec(memory_space=pltpu.VMEM)
    hbm = pl.BlockSpec(memory_space=pl.ANY)
    plan_out, u_out, v_out = pl.pallas_call(
        functools.partial(kernel, W, N, step_base),
        out_shape=(
            pltpu.VMEM((rows, cols), f32),
            pltpu.VMEM((groups, LANES), f32),
            pltpu.VMEM((chunks, LANES), f32),
        ),
        in_specs=[hbm] * 6,
        out_specs=(vmem, vmem, vmem),
        scratch_shapes=[
            pltpu.VMEM((rows, cols), f32),
            pltpu.VMEM((rows, cols), f32),
            pltpu.VMEM((rows, cols), f32),
            pltpu.VMEM((rows, cols), f32),
            pltpu.VMEM((groups, LANES), f32),
            pltpu.VMEM((chunks, LANES), f32),
            pltpu.VMEM((rows, LANES), f32),
            pltpu.VMEM((groups, LANES), f32),
            pltpu.VMEM((ITERS, chunks, LANES), f32),
            pltpu.VMEM((ITERS + 1, chunks, LANES), f32),
            pltpu.VMEM((ITERS, W, chunks, LANES), f32),
            pltpu.VMEM((ITERS, N, groups, LANES), f32),
            pltpu.VMEM((ITERS, W, 1, LANES), f32),
            pltpu.VMEM((ITERS, W, 1, LANES), f32),
            pltpu.VMEM((ITERS, N, 2, LANES), f32),
            dma((2, BLOCKS)), dma((4,)),
            dma((ITERS, W)), dma((ITERS, W)),
            dma((ITERS, N)), dma((ITERS, N)),
            dma((ITERS, W)), dma((ITERS, W)),
            dma((ITERS, W)), dma((ITERS, W)),
            dma((ITERS, N)), dma((ITERS, N)),
        ],
        compiler_params=pltpu.CompilerParams(collective_id=0, has_side_effects=True),
        name="pdhg",
    )(
        cost, plan,
        row_mass.reshape(groups, LANES), col_mass.reshape(chunks, LANES),
        row_dual.reshape(groups, LANES), col_dual.reshape(chunks, LANES),
    )
    return plan_out, u_out.reshape(rows), v_out.reshape(cols)


def solution(mesh):
    in_specs = (
        P("wide", "narrow"),
        P("wide", "narrow"),
        P("wide"),
        P("narrow"),
        P("wide"),
        P("narrow"),
    )
    out_specs = (P("wide", "narrow"), P("wide"), P("narrow"))
    return jax.shard_map(
        functools.partial(shards, mesh.shape["wide"], mesh.shape["narrow"]),
        mesh=mesh, in_specs=in_specs, out_specs=out_specs, check_vma=False)
```

time: 315 us -> 44.5 us (0.14)
  blocking collectives: 284 us -> 0 us
  Pallas kernels: 0 us -> 41.3 us
  other arithmetic: 21.7 us -> 0 us
  between operations: 9.03 us -> 0.64 us
    psum x11 -> x0, blocking collectives: 284 us -> none  [the longest x4 147 us: shards(): col_total = lax.psum(col_local, 'wide')]
    pallas_call x0 -> x1, Pallas kernels: none -> 41.3 us  [shards(): pl.pallas_call(functools.partial(kernel, W, N, step_base), out_shape=(plt...]
    reduce_sum x10 -> x0, other arithmetic: 20.6 us -> none  [the longest x3 12.1 us: shards(): moved = jnp.sum(change * change)]
where the time goes in v2:
time: 44.5 us; the launch traced here: 44.4 us
  Pallas kernels  41.3 us (93%)
  local copies, waits for them, and re-layouts  2.44 us (5%)
  between operations  0.64 us (1%)
    pallas_call x1, Pallas kernels, shards(): pl.pallas_call(functools.partial(kernel, W, N, step_base), out_shape=(plt...  41.3 us
    unnamed x3, local copies, waits for them, and re-layouts  2.44 us

profile of v2, /device:TPU:0, one launch (start us, length us, event | category | flops | bytes accessed | tf_op | source)
XLA Modules:
  0.0 44.4 jit_solution(5751965721523646739)
XLA Ops:
  0.6 41.3 %pdhg.1 = (f32[128,4096]{1,0:T(8,128)S(1)}, f32[1,128]{1,0:T(1,128)S(1)}, f32[32,128]{1,0:T(8,128)S(1)}) custom-call(f32[128,4096]{1,0:T(8,128)} %cost_hbm.1, f32[128,4096]{1,0:T(8,128)} %plan_hbm.1, f32[1,128]{1,0:T(1,128)} %bitcast.10, f32[32,128]{1,0:T(8,128)} %bitcast.8, f32[1,128]{1,0:T(1,128)} %bitcast.11, f32[32,128]{1,0:T(8,128)} %bitcast.9), custom_call_target="tpu_custom_call" | custom-call | tf_op jit(solution)/shard_map/pdhg/pallas_call | solution.py:234
  41.9 1.3 %copy.12 = f32[128,4096]{1,0:T(8,128)} copy(f32[128,4096]{1,0:T(8,128)S(1)} %get-tuple-element.9) | data formatting | bytes 4194304
  43.3 0.5 %copy.13 = f32[128]{0:T(128)} copy(f32[128]{0:T(128)S(1)} %bitcast.7) | data formatting | bytes 1024
  43.8 0.6 %copy.14 = f32[4096]{0:T(1024)} copy(f32[4096]{0:T(1024)S(1)} %bitcast.6) | data formatting | bytes 32768

commit v3 on v2

--- a/solution.py
+++ b/solution.py
@@ -46,7 +46,7 @@
     W, N, step_base,
     cost_hbm, plan_hbm, rmass_hbm, cmass_hbm, u_hbm, v_hbm,
     plan_out, u_out, v_out,
-    cost, plan_a, plan_b, gap, rmass, cmass, ub, ucur, V, CB, RB, RP, RH, MV, SC,
+    cost, plan_a, plan_b, gap, rmass, cmass, ub, ucur, V, CB, fold, RB, RP, RH, MV, SC,
     in_sem, small_sem,
     s1_send, s1_recv, row_send, row_recv, rho_send, rho_recv,
     mv_send, mv_recv, sc_send, sc_recv,
@@ -104,6 +104,18 @@
             axis=0,
         )
 
+    def by_sublane(x):
+        return jnp.sum(x.reshape(rows // 8, 8, LANES), axis=0)
+
+    def keep_columns(c, x):
+        fold[pl.ds(pl.multiple_of(c * 8, 8), 8), :] = by_sublane(x)
+
+    def columns():
+        out = fold[pl.ds(0, chunks, stride=8), :]
+        for i in range(1, 8):
+            out = out + fold[pl.ds(i, chunks, stride=8), :]
+        return out
+
     def lanes_of(c):
         return pl.ds(pl.multiple_of(c * LANES, LANES), LANES)
 
@@ -113,6 +125,7 @@
 
     zero_rows = jnp.zeros((rows, LANES), jnp.float32)
     weight = jnp.full((1, 1), step_base, jnp.float32)
+    tau = jnp.ones((1, LANES), jnp.float32)
     row_old = None
     pending = []
     for k in range(ITERS):
@@ -120,7 +133,6 @@
         old = plan_a if k % 2 == 0 else plan_b
         new = plan_out if last else (plan_b if k % 2 == 0 else plan_a)
         dual = step_base * weight
-        tau = jnp.broadcast_to(step_base / weight, (1, LANES))
 
         if k == 0:
             def first(c, racc, old=old, new=new, tau=tau):
@@ -130,7 +142,7 @@
                     x - tau * (cost[:, lanes] - ub[...] - V[0, pl.ds(c, 1), :]), 0.0)
                 new[:, lanes] = f
                 ext = f + (f - x)
-                CB[0, pl.ds(c, 1), :] = jnp.sum(ext, axis=0, keepdims=True)
+                keep_columns(c, ext)
                 return racc + ext
 
             racc = zero_rows
@@ -139,18 +151,20 @@
                     copy.wait()
                 racc = lax.fori_loop(
                     b * per_block, (b + 1) * per_block, first, racc, unroll=2)
-            RB[0, w] = CB[0]
+            RB[0, w] = columns()
             pl.semaphore_wait(barrier, W - 1 + N - 1)
         else:
             def step(c, racc, k=k, old=old, new=new, tau=tau):
                 lanes = lanes_of(c)
                 f = jnp.maximum(old[:, lanes] - tau * gap[:, lanes], 0.0)
                 new[:, lanes] = f
-                CB[k + 1, pl.ds(c, 1), :] = jnp.sum(f, axis=0, keepdims=True)
+                keep_columns(c, f)
                 return racc + f
 
-            racc = lax.fori_loop(0, chunks, step, zero_rows, unroll=4)
-            RB[k, w] = 2.0 * CB[k + 1] - CB[k]
+            racc = lax.fori_loop(0, chunks, step, zero_rows, unroll=32)
+            fresh_cols = columns()
+            RB[k, w] = 2.0 * fresh_cols - CB[...]
+            CB[...] = fresh_cols
 
         sent, col_waits = exchange(RB, k, w, wide_peers, s1_send, s1_recv)
         pending += sent
@@ -165,20 +179,21 @@
                 lanes = lanes_of(c)
                 f = new[:, lanes]
                 ch = f - old[:, lanes]
-                sq = jnp.sum((ch * ch).reshape(rows // 8, 8, LANES), axis=0)
+                sq = by_sublane(ch * ch)
                 if k:
                     return (carry[0] + sq,)
-                CB[1, pl.ds(c, 1), :] = jnp.sum(f, axis=0, keepdims=True)
+                keep_columns(c, f)
                 return carry[0] + sq, carry[1] + f
 
             start = (jnp.zeros((8, LANES), jnp.float32),)
             out = lax.fori_loop(
                 0, chunks, change, start if k else start + (zero_rows,), unroll=2)
-            MV[k, w] = jnp.sum(out[0], axis=0, keepdims=True)
-            sent, mv_waits = exchange(MV, k, w, wide_peers, mv_send, mv_recv)
+            MV[k, n] = jnp.sum(out[0], axis=0, keepdims=True)
+            sent, mv_waits = exchange(MV, k, n, narrow_peers, mv_send, mv_recv)
             pending += sent
             if k == 0:
                 row_old = to_lanes(out[1])
+                CB[...] = columns()
 
         arrived(row_waits)
         u_old = ucur[...]
@@ -186,13 +201,13 @@
         if last:
             u_out[...] = u_new
         else:
-            RH[k, w] = jnp.sum((u_new - u_old) ** 2, axis=0, keepdims=True)
+            RH[k, w, 0:1, :] = jnp.sum((u_new - u_old) ** 2, axis=0, keepdims=True)
+            arrived(mv_waits)
+            RH[k, w, 1:2, :] = total_of(MV, k, N)
             sent, rho_waits = exchange(RH, k, w, wide_peers, rho_send, rho_recv)
             pending += sent
             ucur[...] = u_new
             spread(u_new)
-            arrived(mv_waits)
-            SC[k, n, 1:2, :] = total_of(MV, k, W)
 
         arrived(col_waits)
         v_old = V[k]
@@ -200,7 +215,7 @@
         if last:
             v_out[...] = v_new
             continue
-        SC[k, n, 0:1, :] = jnp.sum((v_new - v_old) ** 2, axis=0, keepdims=True)
+        SC[k, n] = jnp.sum((v_new - v_old) ** 2, axis=0, keepdims=True)
         V[k + 1] = v_new
         sent, sc_waits = exchange(SC, k, n, narrow_peers, sc_send, sc_recv)
         pending += sent
@@ -212,14 +227,31 @@
 
         lax.fori_loop(0, chunks, reduce_cost, 0, unroll=2)
         arrived(rho_waits)
-        rho = total_of(RH, k, W)
+        known = jnp.sum(total_of(RH, k, W), axis=1, keepdims=True)
+        known_dual = known[0:1] + 1.0
+        per_moved = 1.0 / (known[1:2] + 1.0)
         arrived(sc_waits)
-        both = total_of(SC, k, N)
-        dual_moved = jnp.sum(rho + both[0:1], axis=1, keepdims=True)
-        moved = jnp.sum(both[1:2], axis=1, keepdims=True)
-        weight = jnp.sqrt(weight * jnp.sqrt((dual_moved + 1.0) / (moved + 1.0)))
+        col_square = jnp.sum(total_of(SC, k, N), axis=1, keepdims=True)
+        square = weight * jnp.sqrt((known_dual + col_square) * per_moved)
+        tau = jnp.broadcast_to(step_base * lax.rsqrt(square), (1, LANES))
+        weight = jnp.sqrt(square)
     for copy in pending:
         copy.wait_send()
+
+
+def store(plan, u, v, plan_hbm, u_hbm, v_hbm, sem):
+    height = plan.shape[0] // BLOCKS
+    copies = [
+        pltpu.make_async_copy(u, u_hbm, sem.at[BLOCKS]),
+        pltpu.make_async_copy(v, v_hbm, sem.at[BLOCKS + 1]),
+    ]
+    for b in range(BLOCKS):
+        sl = pl.ds(b * height, height)
+        copies.append(pltpu.make_async_copy(plan.at[sl], plan_hbm.at[sl], sem.at[b]))
+    for copy in copies:
+        copy.start()
+    for copy in copies:
+        copy.wait()
 
 
 def shards(W, N, cost, plan, row_mass, col_mass, row_dual, col_dual):
@@ -250,17 +282,18 @@
             pltpu.VMEM((rows, LANES), f32),
             pltpu.VMEM((groups, LANES), f32),
             pltpu.VMEM((ITERS, chunks, LANES), f32),
-            pltpu.VMEM((ITERS + 1, chunks, LANES), f32),
+            pltpu.VMEM((chunks, LANES), f32),
+            pltpu.VMEM((chunks * 8, LANES), f32),
             pltpu.VMEM((ITERS, W, chunks, LANES), f32),
             pltpu.VMEM((ITERS, N, groups, LANES), f32),
-            pltpu.VMEM((ITERS, W, 1, LANES), f32),
-            pltpu.VMEM((ITERS, W, 1, LANES), f32),
-            pltpu.VMEM((ITERS, N, 2, LANES), f32),
+            pltpu.VMEM((ITERS, W, 2, LANES), f32),
+            pltpu.VMEM((ITERS, N, 1, LANES), f32),
+            pltpu.VMEM((ITERS, N, 1, LANES), f32),
             dma((2, BLOCKS)), dma((4,)),
             dma((ITERS, W)), dma((ITERS, W)),
             dma((ITERS, N)), dma((ITERS, N)),
             dma((ITERS, W)), dma((ITERS, W)),
-            dma((ITERS, W)), dma((ITERS, W)),
+            dma((ITERS, N)), dma((ITERS, N)),
             dma((ITERS, N)), dma((ITERS, N)),
         ],
         compiler_params=pltpu.CompilerParams(collective_id=0, has_side_effects=True),
@@ -270,6 +303,19 @@
         row_mass.reshape(groups, LANES), col_mass.reshape(chunks, LANES),
         row_dual.reshape(groups, LANES), col_dual.reshape(chunks, LANES),
     )
+    keep = functools.partial(pltpu.with_memory_space_constraint, memory_space=pltpu.VMEM)
+    plan_out, u_out, v_out = pl.pallas_call(
+        store,
+        out_shape=(
+            jax.ShapeDtypeStruct((rows, cols), f32),
+            jax.ShapeDtypeStruct((groups, LANES), f32),
+            jax.ShapeDtypeStruct((chunks, LANES), f32),
+        ),
+        in_specs=[vmem, vmem, vmem],
+        out_specs=(hbm, hbm, hbm),
+        scratch_shapes=[dma((BLOCKS + 2,))],
+        name="store",
+    )(keep(plan_out), keep(u_out), keep(v_out))
     return plan_out, u_out.reshape(rows), v_out.reshape(cols)
 
 

time: 44.5 us -> 40.5 us (0.910)
  local copies, waits for them, and re-layouts: 2.44 us -> 0 us
  Pallas kernels: 41.3 us -> 39.7 us
    pallas_call x1, Pallas kernels: 41.3 us -> 38.3 us  [shards(): pl.pallas_call(functools.partial(kernel, W, N, step_base), out_shape=(plt...]
    unnamed x3 -> x0, local copies, waits for them, and re-layouts: 2.44 us -> none
    pallas_call x0 -> x1, Pallas kernels: none -> 1.4 us  [shards(): pl.pallas_call(store, out_shape=(jax.ShapeDtypeStruct((rows, cols), f32),...]
where the time goes in v3:
time: 40.5 us; the launch traced here: 40.3 us
  Pallas kernels  39.7 us (98%)
  between operations  0.64 us (2%)
    pallas_call x1, Pallas kernels, shards(): pl.pallas_call(functools.partial(kernel, W, N, step_base), out_shape=(plt...  38.3 us
    pallas_call x1, Pallas kernels, shards(): pl.pallas_call(store, out_shape=(jax.ShapeDtypeStruct((rows, cols), f32),...  1.4 us

profile of v3, /device:TPU:0, one launch (start us, length us, event | category | flops | bytes accessed | tf_op | source)
XLA Modules:
  0.0 40.3 jit_solution(2650446339797988291)
XLA Ops:
  0.6 38.3 %pdhg.1 = (f32[128,4096]{1,0:T(8,128)S(1)}, f32[1,128]{1,0:T(1,128)S(1)}, f32[32,128]{1,0:T(8,128)S(1)}) custom-call(f32[128,4096]{1,0:T(8,128)} %cost_hbm.1, f32[128,4096]{1,0:T(8,128)} %plan_hbm.1, f32[1,128]{1,0:T(1,128)} %bitcast.8, f32[32,128]{1,0:T(8,128)} %bitcast.6, f32[1,128]{1,0:T(1,128)} %bitcast.9, f32[32,128]{1,0:T(8,128)} %bitcast.7), custom_call_target="tpu_custom_call" | custom-call | tf_op jit(solution)/shard_map/pdhg/pallas_call | solution.py:266
  38.9 1.4 %store.1 = (f32[128,4096]{1,0:T(8,128)}, f32[1,128]{1,0:T(1,128)}, f32[32,128]{1,0:T(8,128)}) custom-call(f32[128,4096]{1,0:T(8,128)S(1)} %get-tuple-element.9.plan, f32[1,128]{1,0:T(1,128)S(1)} %get-tuple-element.10.u, f32[32,128]{1,0:T(8,128)S(1)} %get-tuple-element.11.v), custom_call_target="tpu_custom_call" | custom-call | tf_op jit(solution)/shard_map/store/pallas_call | solution.py:307

commit v4 on v3

--- a/solution.py
+++ b/solution.py
@@ -60,7 +60,7 @@
     n = lax.axis_index("narrow")
 
     wide_peers = []
-    for d in range(W - 1, 0, -1):
+    for d in sorted(range(1, W), key=lambda d: (d % 2 == 0, d)):
         to = lax.rem(w + d, W)
         wide_peers.append((to, lax.rem(w + W - d, W), (to, n)))
     narrow_peers = []
@@ -187,7 +187,7 @@
 
             start = (jnp.zeros((8, LANES), jnp.float32),)
             out = lax.fori_loop(
-                0, chunks, change, start if k else start + (zero_rows,), unroll=2)
+                0, chunks, change, start if k else start + (zero_rows,), unroll=8)
             MV[k, n] = jnp.sum(out[0], axis=0, keepdims=True)
             sent, mv_waits = exchange(MV, k, n, narrow_peers, mv_send, mv_recv)
             pending += sent
@@ -225,7 +225,7 @@
             gap[:, lanes] = cost[:, lanes] - ub[...] - V[k + 1, pl.ds(c, 1), :]
             return carry
 
-        lax.fori_loop(0, chunks, reduce_cost, 0, unroll=2)
+        lax.fori_loop(0, chunks, reduce_cost, 0, unroll=8)
         arrived(rho_waits)
         known = jnp.sum(total_of(RH, k, W), axis=1, keepdims=True)
         known_dual = known[0:1] + 1.0

time: 40.5 us -> 38.9 us (0.960)
  Pallas kernels: 39.7 us -> 38.1 us
    pallas_call x1, Pallas kernels: 38.3 us -> 36.7 us  [shards(): pl.pallas_call(functools.partial(kernel, W, N, step_base), out_shape=(plt...]
where the time goes in v4:
time: 38.9 us; the launch traced here: 38.8 us
  Pallas kernels  38.1 us (98%)
  between operations  0.64 us (2%)
    pallas_call x1, Pallas kernels, shards(): pl.pallas_call(functools.partial(kernel, W, N, step_base), out_shape=(plt...  36.7 us
    pallas_call x1, Pallas kernels, shards(): pl.pallas_call(store, out_shape=(jax.ShapeDtypeStruct((rows, cols), f32),...  1.4 us

profile of v4, /device:TPU:0, one launch (start us, length us, event | category | flops | bytes accessed | tf_op | source)
XLA Modules:
  0.0 38.8 jit_solution(3858693272565109791)
XLA Ops:
  0.6 36.7 %pdhg.1 = (f32[128,4096]{1,0:T(8,128)S(1)}, f32[1,128]{1,0:T(1,128)S(1)}, f32[32,128]{1,0:T(8,128)S(1)}) custom-call(f32[128,4096]{1,0:T(8,128)} %cost_hbm.1, f32[128,4096]{1,0:T(8,128)} %plan_hbm.1, f32[1,128]{1,0:T(1,128)} %bitcast.8, f32[32,128]{1,0:T(8,128)} %bitcast.6, f32[1,128]{1,0:T(1,128)} %bitcast.9, f32[32,128]{1,0:T(8,128)} %bitcast.7), custom_call_target="tpu_custom_call" | custom-call | tf_op jit(solution)/shard_map/pdhg/pallas_call | solution.py:266
  37.4 1.4 %store.1 = (f32[128,4096]{1,0:T(8,128)}, f32[1,128]{1,0:T(1,128)}, f32[32,128]{1,0:T(8,128)}) custom-call(f32[128,4096]{1,0:T(8,128)S(1)} %get-tuple-element.9.plan, f32[1,128]{1,0:T(1,128)S(1)} %get-tuple-element.10.u, f32[32,128]{1,0:T(8,128)S(1)} %get-tuple-element.11.v), custom_call_target="tpu_custom_call" | custom-call | tf_op jit(solution)/shard_map/store/pallas_call | solution.py:307
